TPU v7x, 32 devices: a whole 2x2x4 slice. The times are simulated.
32 devices in a mesh: gx: 8 (over z, x), gy: 2 (over y), gz: 2 (over core).
Axes of the slice: x: 2, y: 2, z: 4, core: 2. Of those that a mesh axis runs over, the one named last changes fastest.
Arguments:
- velocity_term: float32 [32, 64, 256], P('gx', 'gy', 'gz'), may hold values from 0.05 to 0.2
- model_step: float32 [32, 64, 256], P('gx', 'gy', 'gz'), may hold values from -6 to 6
- background: bfloat16 [4, 32, 64, 256], P(None, 'gx', 'gy', 'gz'), may hold values from -6 to 6
- receivers: int32 [3, 256], replicated, may hold values from 0 to 255, as said below
- checkpoints: int32 [16], replicated, may hold values from 0 to 3, as said below
Outputs:
- image: float32 [32, 64, 256], P('gx', 'gy', 'gz')
- traces: float32 [16, 256], replicated
- column_image: float32 [32, 64], P('gx', 'gy')
- wavefield: float32 [32, 64, 256], P('gx', 'gy', 'gz')
Inputs may be any that keep to these rules, and one draw needn't show every extreme that they name: receivers[0] indexes the first lateral dimension (below 32), receivers[1] the second (below 64), receivers[2] depth (below 256). `checkpoints`: never falling over the time steps, beginning at 0 and ending at 3.
All inputs are finite; a program needn't handle non-finite values.
Results may differ from a plain program's by a relative error of at most 0.0003.
Values sent between devices are 32-bit elements; how exact they have to be, the bound alone decides.
A program may use at most 64 MiB of HBM per device.

v0:
```python
import jax
import jax.numpy as jnp
from jax import lax
from jax.sharding import PartitionSpec as P

near_coef = 4.0 / 3.0
far_coef = -1.0 / 12.0
center_coef = -2.5


def with_halo(block, sides, width, periodic):
    for axis, dim in sides:
        count = lax.axis_size(axis)
        forward = [(i, i + 1) for i in range(count - 1)]
        if periodic:
            forward.append((count - 1, 0))
        backward = [(target, source) for source, target in forward]
        low = lax.ppermute(
            lax.slice_in_dim(block, block.shape[dim] - width, None, axis=dim), axis, forward
        )
        high = lax.ppermute(lax.slice_in_dim(block, 0, width, axis=dim), axis, backward)
        block = jnp.concatenate([low, block, high], axis=dim)
    return block


def along(padded, dim):
    count = padded.shape[dim]
    first = lax.slice_in_dim(padded, 3, count - 1, axis=dim) + lax.slice_in_dim(
        padded, 1, count - 3, axis=dim
    )
    second = lax.slice_in_dim(padded, 4, count, axis=dim) + lax.slice_in_dim(
        padded, 0, count - 4, axis=dim
    )
    return near_coef * first + far_coef * second


def laplace(field):
    side = with_halo(field, (("gx", 0), ("gy", 1)), 2, True)
    deep = with_halo(field, (("gz", 2),), 2, False)
    x_pad = side[:, 2:-2, :]
    y_pad = side[2:-2, :, :]
    return 3.0 * center_coef * field + along(x_pad, 0) + along(y_pad, 1) + along(deep, 2)


def sample_row(samples, field, step, clip_x, clip_y, clip_z, inside):
    values = field[clip_x, clip_y, clip_z] * inside
    return lax.dynamic_update_index_in_dim(samples, values, step, 0)


def on_device(velocity_term, model_step, background, receivers, checkpoints):
    size_x, size_y, size_z = model_step.shape
    steps = checkpoints.shape[0]
    local_x = receivers[0] - lax.axis_index("gx") * size_x
    local_y = receivers[1] - lax.axis_index("gy") * size_y
    local_z = receivers[2] - lax.axis_index("gz") * size_z
    inside = (
        (local_x >= 0)
        & (local_x < size_x)
        & (local_y >= 0)
        & (local_y < size_y)
        & (local_z >= 0)
        & (local_z < size_z)
    )
    inside = inside.astype(jnp.float32)
    clip_x = jnp.clip(local_x, 0, size_x - 1)
    clip_y = jnp.clip(local_y, 0, size_y - 1)
    clip_z = jnp.clip(local_z, 0, size_z - 1)
    zeros = jnp.zeros(model_step.shape, jnp.float32)
    record = jnp.zeros((steps, receivers.shape[1]), jnp.float32)

    def forward(step, carry):
        previous, current, samples = carry
        accel = lax.dynamic_index_in_dim(background, checkpoints[step], 0, keepdims=False).astype(
            jnp.float32
        )
        following = 2.0 * current - previous + velocity_term * laplace(current) + model_step * accel
        samples = sample_row(samples, following, step, clip_x, clip_y, clip_z, inside)
        return (current, following, samples)

    previous, current, record = lax.fori_loop(0, steps, forward, (zeros, zeros, record))
    traces = lax.psum(record, ("gx", "gy", "gz"))

    def adjoint_step(back, carry):
        later_two, later, image = carry
        step = steps - 1 - back
        accel = lax.dynamic_index_in_dim(background, checkpoints[step], 0, keepdims=False).astype(
            jnp.float32
        )
        adjoint = 2.0 * later - later_two + laplace(velocity_term * later)
        inject = lax.dynamic_index_in_dim(traces, step, 0, keepdims=False) * inside
        adjoint = adjoint.at[clip_x, clip_y, clip_z].add(inject)
        return (later, adjoint, image + adjoint * accel)

    later_two, later, image = lax.fori_loop(0, steps, adjoint_step, (zeros, zeros, zeros))
    depth_total = size_z * lax.axis_size("gz")
    column_image = lax.psum(jnp.sum(image, axis=2), "gz") / depth_total
    return (image, traces, column_image, current)


def solution(mesh):
    placed = (P("gx", "gy", "gz"), P("gx", "gy", "gz"), P(None, "gx", "gy", "gz"), P(), P())
    return jax.shard_map(
        on_device,
        mesh=mesh,
        in_specs=placed,
        out_specs=(P("gx", "gy", "gz"), P(), P("gx", "gy"), P("gx", "gy", "gz")),
        check_vma=False,
    )
```

profile of v0, /device:TPU:1, one launch (start us, length us, event | category | flops | bytes accessed | tf_op | source)
XLA Modules:
  0.0 776.5 jit_solution(5892147536605101205)
XLA Ops:
  3.0 263.4 %while.38 = (s32[]{:T(128)}, f32[4,32,128]{2,1,0:T(8,128)S(1)}, f32[4,32,128]{2,1,0:T(8,128)S(1)}, f32[16,256]{1,0:T(8,128)S(1)}, f32[4,32,128]{2,1,0:T(8,128)S(...) while((s32[]{:T(128)}, f32[4,32,128]{2,1,0:T(8,128)S(1)}, ...), condition=%wide.region_1.2_spmd.clone, body=%wide.region_0.1_spmd.clone.sunk | while | flops 782854 | bytes 1602017 | solution.py:80
  20.4 4.1 collective-permute-start.1
  36.8 4.1 collective-permute-start.1
  53.2 4.1 collective-permute-start.1
  69.6 4.1 collective-permute-start.1
  86.0 4.1 collective-permute-start.1
  200.8 4.1 collective-permute-start.1
  217.2 4.1 collective-permute-start.1
  233.6 4.1 collective-permute-start.1
  250.0 4.1 collective-permute-start.1
  266.4 37.1 %psum.14 = f32[16,256]{1,0:T(8,128)S(1)} all-reduce(f32[16,256]{1,0:T(8,128)S(1)} %get-tuple-element.490), channel_id=1, replica_groups=mesh['gx'=8,'gy'=2,'gz'=2] {'gx','gy','gz'}, use_global_device_ids=true, to_apply=%region_2.3 | all-reduce | flops 4096 | bytes 32768 | tf_op jit(solution)/shard_map/psum | solution.py:81
  303.5 469.7 %while.39 = (s32[]{:T(128)}, f32[4,32,128]{2,1,0:T(8,128)S(1)}, f32[4,32,128]{2,1,0:T(8,128)S(1)}, f32[4,32,128]{2,1,0:T(8,128)S(1)}, f32[4,32,128]{2,1,0:T(8,12...) while((s32[]{:T(128)}, f32[4,32,128]{2,1,0:T(8,128)S(1)}, ...), condition=%wide.region_5.6_spmd.clone, body=%wide.region_3.5_spmd.clone.sunk | while | flops 784650 | bytes 1668603 | solution.py:94
  318.2 15.4 %scatter_fusion = f32[4,32,128]{2,1,0:T(8,128)S(1)} fusion(f32[4,32,128]{2,1,0:T(8,128)S(1)} %fusion.75, s32[256]{0:T(256)S(1)} %bitcast.50, f32[256]{0:T(256)S(1)} %mul.354), kind=kCustom, calls=%fused_computation.1.clone.clone.1 | custom fusion | flops 256 | bytes 6144 | tf_op jit(solution)/shard_map/while/body/eval_jaxpr/scatter-add | solution.py:91
  334.4 4.1 collective-permute-start.7
  347.5 15.4 %scatter_fusion = f32[4,32,128]{2,1,0:T(8,128)S(1)} fusion(f32[4,32,128]{2,1,0:T(8,128)S(1)} %fusion.75, s32[256]{0:T(256)S(1)} %bitcast.50, f32[256]{0:T(256)S(1)} %mul.354), kind=kCustom, calls=%fused_computation.1.clone.clone.1 | custom fusion | flops 256 | bytes 6144 | tf_op jit(solution)/shard_map/while/body/eval_jaxpr/scatter-add | solution.py:91
  376.7 15.4 %scatter_fusion = f32[4,32,128]{2,1,0:T(8,128)S(1)} fusion(f32[4,32,128]{2,1,0:T(8,128)S(1)} %fusion.75, s32[256]{0:T(256)S(1)} %bitcast.50, f32[256]{0:T(256)S(1)} %mul.354), kind=kCustom, calls=%fused_computation.1.clone.clone.1 | custom fusion | flops 256 | bytes 6144 | tf_op jit(solution)/shard_map/while/body/eval_jaxpr/scatter-add | solution.py:91
  393.0 4.1 collective-permute-start.7
  406.0 15.4 %scatter_fusion = f32[4,32,128]{2,1,0:T(8,128)S(1)} fusion(f32[4,32,128]{2,1,0:T(8,128)S(1)} %fusion.75, s32[256]{0:T(256)S(1)} %bitcast.50, f32[256]{0:T(256)S(1)} %mul.354), kind=kCustom, calls=%fused_computation.1.clone.clone.1 | custom fusion | flops 256 | bytes 6144 | tf_op jit(solution)/shard_map/while/body/eval_jaxpr/scatter-add | solution.py:91
  422.3 4.1 collective-permute-start.7
  435.2 15.4 %scatter_fusion = f32[4,32,128]{2,1,0:T(8,128)S(1)} fusion(f32[4,32,128]{2,1,0:T(8,128)S(1)} %fusion.75, s32[256]{0:T(256)S(1)} %bitcast.50, f32[256]{0:T(256)S(1)} %mul.354), kind=kCustom, calls=%fused_computation.1.clone.clone.1 | custom fusion | flops 256 | bytes 6144 | tf_op jit(solution)/shard_map/while/body/eval_jaxpr/scatter-add | solution.py:91
  464.5 15.4 %scatter_fusion = f32[4,32,128]{2,1,0:T(8,128)S(1)} fusion(f32[4,32,128]{2,1,0:T(8,128)S(1)} %fusion.75, s32[256]{0:T(256)S(1)} %bitcast.50, f32[256]{0:T(256)S(1)} %mul.354), kind=kCustom, calls=%fused_computation.1.clone.clone.1 | custom fusion | flops 256 | bytes 6144 | tf_op jit(solution)/shard_map/while/body/eval_jaxpr/scatter-add | solution.py:91
  480.8 4.1 collective-permute-start.7
  493.7 15.4 %scatter_fusion = f32[4,32,128]{2,1,0:T(8,128)S(1)} fusion(f32[4,32,128]{2,1,0:T(8,128)S(1)} %fusion.75, s32[256]{0:T(256)S(1)} %bitcast.50, f32[256]{0:T(256)S(1)} %mul.354), kind=kCustom, calls=%fused_computation.1.clone.clone.1 | custom fusion | flops 256 | bytes 6144 | tf_op jit(solution)/shard_map/while/body/eval_jaxpr/scatter-add | solution.py:91
  523.0 15.4 %scatter_fusion = f32[4,32,128]{2,1,0:T(8,128)S(1)} fusion(f32[4,32,128]{2,1,0:T(8,128)S(1)} %fusion.75, s32[256]{0:T(256)S(1)} %bitcast.50, f32[256]{0:T(256)S(1)} %mul.354), kind=kCustom, calls=%fused_computation.1.clone.clone.1 | custom fusion | flops 256 | bytes 6144 | tf_op jit(solution)/shard_map/while/body/eval_jaxpr/scatter-add | solution.py:91
  552.2 15.4 %scatter_fusion = f32[4,32,128]{2,1,0:T(8,128)S(1)} fusion(f32[4,32,128]{2,1,0:T(8,128)S(1)} %fusion.75, s32[256]{0:T(256)S(1)} %bitcast.50, f32[256]{0:T(256)S(1)} %mul.354), kind=kCustom, calls=%fused_computation.1.clone.clone.1 | custom fusion | flops 256 | bytes 6144 | tf_op jit(solution)/shard_map/while/body/eval_jaxpr/scatter-add | solution.py:91
  581.5 15.4 %scatter_fusion = f32[4,32,128]{2,1,0:T(8,128)S(1)} fusion(f32[4,32,128]{2,1,0:T(8,128)S(1)} %fusion.75, s32[256]{0:T(256)S(1)} %bitcast.50, f32[256]{0:T(256)S(1)} %mul.354), kind=kCustom, calls=%fused_computation.1.clone.clone.1 | custom fusion | flops 256 | bytes 6144 | tf_op jit(solution)/shard_map/while/body/eval_jaxpr/scatter-add | solution.py:91
  610.8 15.4 %scatter_fusion = f32[4,32,128]{2,1,0:T(8,128)S(1)} fusion(f32[4,32,128]{2,1,0:T(8,128)S(1)} %fusion.75, s32[256]{0:T(256)S(1)} %bitcast.50, f32[256]{0:T(256)S(1)} %mul.354), kind=kCustom, calls=%fused_computation.1.clone.clone.1 | custom fusion | flops 256 | bytes 6144 | tf_op jit(solution)/shard_map/while/body/eval_jaxpr/scatter-add | solution.py:91
  640.0 15.4 %scatter_fusion = f32[4,32,128]{2,1,0:T(8,128)S(1)} fusion(f32[4,32,128]{2,1,0:T(8,128)S(1)} %fusion.75, s32[256]{0:T(256)S(1)} %bitcast.50, f32[256]{0:T(256)S(1)} %mul.354), kind=kCustom, calls=%fused_computation.1.clone.clone.1 | custom fusion | flops 256 | bytes 6144 | tf_op jit(solution)/shard_map/while/body/eval_jaxpr/scatter-add | solution.py:91
  669.3 15.4 %scatter_fusion = f32[4,32,128]{2,1,0:T(8,128)S(1)} fusion(f32[4,32,128]{2,1,0:T(8,128)S(1)} %fusion.75, s32[256]{0:T(256)S(1)} %bitcast.50, f32[256]{0:T(256)S(1)} %mul.354), kind=kCustom, calls=%fused_computation.1.clone.clone.1 | custom fusion | flops 256 | bytes 6144 | tf_op jit(solution)/shard_map/while/body/eval_jaxpr/scatter-add | solution.py:91
  698.5 15.4 %scatter_fusion = f32[4,32,128]{2,1,0:T(8,128)S(1)} fusion(f32[4,32,128]{2,1,0:T(8,128)S(1)} %fusion.75, s32[256]{0:T(256)S(1)} %bitcast.50, f32[256]{0:T(256)S(1)} %mul.354), kind=kCustom, calls=%fused_computation.1.clone.clone.1 | custom fusion | flops 256 | bytes 6144 | tf_op jit(solution)/shard_map/while/body/eval_jaxpr/scatter-add | solution.py:91
  727.8 15.4 %scatter_fusion = f32[4,32,128]{2,1,0:T(8,128)S(1)} fusion(f32[4,32,128]{2,1,0:T(8,128)S(1)} %fusion.75, s32[256]{0:T(256)S(1)} %bitcast.50, f32[256]{0:T(256)S(1)} %mul.354), kind=kCustom, calls=%fused_computation.1.clone.clone.1 | custom fusion | flops 256 | bytes 6144 | tf_op jit(solution)/shard_map/while/body/eval_jaxpr/scatter-add | solution.py:91
  757.0 15.4 %scatter_fusion = f32[4,32,128]{2,1,0:T(8,128)S(1)} fusion(f32[4,32,128]{2,1,0:T(8,128)S(1)} %fusion.75, s32[256]{0:T(256)S(1)} %bitcast.50, f32[256]{0:T(256)S(1)} %mul.354), kind=kCustom, calls=%fused_computation.1.clone.clone.1 | custom fusion | flops 256 | bytes 6144 | tf_op jit(solution)/shard_map/while/body/eval_jaxpr/scatter-add | solution.py:91
  (792 shorter events, 371.4 us)
Async XLA Ops:
  3.0 9.7 %collective-permute-start = (f32[2,32,128]{2,1,0:T(8,128)S(1)}, f32[2,32,128]{2,1,0:T(8,128)S(1)}, u32[]{:S(2)}, u32[]{:S(2)}) collective-permute-start(f32[2,32,128]{2,1,0:T(8,128)S(1)} %get-tuple-element.780), channel_id=1, source_target_pairs={{0,4},{4,8},{8,12},{12,16},{16,20},{20,24},{24,28},{28,0},{1,5},{5... | collective-permute-start | bytes 98312 | tf_op jit(solution)/shard_map/while/body/eval_jaxpr/ppermute | solution.py:18
  20.4 8.8 %collective-permute-start = (f32[2,32,128]{2,1,0:T(8,128)S(1)}, f32[2,32,128]{2,1,0:T(8,128)S(1)}, u32[]{:S(2)}, u32[]{:S(2)}) collective-permute-start(f32[2,32,128]{2,1,0:T(8,128)S(1)} %get-tuple-element.780), channel_id=1, source_target_pairs={{0,4},{4,8},{8,12},{12,16},{16,20},{20,24},{24,28},{28,0},{1,5},{5... | collective-permute-start | bytes 98312 | tf_op jit(solution)/shard_map/while/body/eval_jaxpr/ppermute | solution.py:18
  20.4 8.7 %collective-permute-start.1 = (f32[2,32,128]{2,1,0:T(8,128)S(1)}, f32[2,32,128]{2,1,0:T(8,128)S(1)}, u32[]{:S(2)}, u32[]{:S(2)}) collective-permute-start(f32[2,32,128]{2,1,0:T(8,128)S(1)} %get-tuple-element.781), channel_id=1, source_target_pairs={{4,0},{8,4},{12,8},{16,12},{20,16},{24,20},{28,24},{0,28},{5,1},{9... | collective-permute-start | bytes 98312 | tf_op jit(solution)/shard_map/while/body/eval_jaxpr/ppermute | solution.py:21
  36.8 8.8 %collective-permute-start = (f32[2,32,128]{2,1,0:T(8,128)S(1)}, f32[2,32,128]{2,1,0:T(8,128)S(1)}, u32[]{:S(2)}, u32[]{:S(2)}) collective-permute-start(f32[2,32,128]{2,1,0:T(8,128)S(1)} %get-tuple-element.780), channel_id=1, source_target_pairs={{0,4},{4,8},{8,12},{12,16},{16,20},{20,24},{24,28},{28,0},{1,5},{5... | collective-permute-start | bytes 98312 | tf_op jit(solution)/shard_map/while/body/eval_jaxpr/ppermute | solution.py:18
  36.8 8.7 %collective-permute-start.1 = (f32[2,32,128]{2,1,0:T(8,128)S(1)}, f32[2,32,128]{2,1,0:T(8,128)S(1)}, u32[]{:S(2)}, u32[]{:S(2)}) collective-permute-start(f32[2,32,128]{2,1,0:T(8,128)S(1)} %get-tuple-element.781), channel_id=1, source_target_pairs={{4,0},{8,4},{12,8},{16,12},{20,16},{24,20},{28,24},{0,28},{5,1},{9... | collective-permute-start | bytes 98312 | tf_op jit(solution)/shard_map/while/body/eval_jaxpr/ppermute | solution.py:21
  53.2 8.8 %collective-permute-start = (f32[2,32,128]{2,1,0:T(8,128)S(1)}, f32[2,32,128]{2,1,0:T(8,128)S(1)}, u32[]{:S(2)}, u32[]{:S(2)}) collective-permute-start(f32[2,32,128]{2,1,0:T(8,128)S(1)} %get-tuple-element.780), channel_id=1, source_target_pairs={{0,4},{4,8},{8,12},{12,16},{16,20},{20,24},{24,28},{28,0},{1,5},{5... | collective-permute-start | bytes 98312 | tf_op jit(solution)/shard_map/while/body/eval_jaxpr/ppermute | solution.py:18
  53.2 8.7 %collective-permute-start.1 = (f32[2,32,128]{2,1,0:T(8,128)S(1)}, f32[2,32,128]{2,1,0:T(8,128)S(1)}, u32[]{:S(2)}, u32[]{:S(2)}) collective-permute-start(f32[2,32,128]{2,1,0:T(8,128)S(1)} %get-tuple-element.781), channel_id=1, source_target_pairs={{4,0},{8,4},{12,8},{16,12},{20,16},{24,20},{28,24},{0,28},{5,1},{9... | collective-permute-start | bytes 98312 | tf_op jit(solution)/shard_map/while/body/eval_jaxpr/ppermute | solution.py:21
  69.6 8.8 %collective-permute-start = (f32[2,32,128]{2,1,0:T(8,128)S(1)}, f32[2,32,128]{2,1,0:T(8,128)S(1)}, u32[]{:S(2)}, u32[]{:S(2)}) collective-permute-start(f32[2,32,128]{2,1,0:T(8,128)S(1)} %get-tuple-element.780), channel_id=1, source_target_pairs={{0,4},{4,8},{8,12},{12,16},{16,20},{20,24},{24,28},{28,0},{1,5},{5... | collective-permute-start | bytes 98312 | tf_op jit(solution)/shard_map/while/body/eval_jaxpr/ppermute | solution.py:18
  69.6 8.7 %collective-permute-start.1 = (f32[2,32,128]{2,1,0:T(8,128)S(1)}, f32[2,32,128]{2,1,0:T(8,128)S(1)}, u32[]{:S(2)}, u32[]{:S(2)}) collective-permute-start(f32[2,32,128]{2,1,0:T(8,128)S(1)} %get-tuple-element.781), channel_id=1, source_target_pairs={{4,0},{8,4},{12,8},{16,12},{20,16},{24,20},{28,24},{0,28},{5,1},{9... | collective-permute-start | bytes 98312 | tf_op jit(solution)/shard_map/while/body/eval_jaxpr/ppermute | solution.py:21
  86.0 8.8 %collective-permute-start = (f32[2,32,128]{2,1,0:T(8,128)S(1)}, f32[2,32,128]{2,1,0:T(8,128)S(1)}, u32[]{:S(2)}, u32[]{:S(2)}) collective-permute-start(f32[2,32,128]{2,1,0:T(8,128)S(1)} %get-tuple-element.780), channel_id=1, source_target_pairs={{0,4},{4,8},{8,12},{12,16},{16,20},{20,24},{24,28},{28,0},{1,5},{5... | collective-permute-start | bytes 98312 | tf_op jit(solution)/shard_map/while/body/eval_jaxpr/ppermute | solution.py:18
  86.0 8.7 %collective-permute-start.1 = (f32[2,32,128]{2,1,0:T(8,128)S(1)}, f32[2,32,128]{2,1,0:T(8,128)S(1)}, u32[]{:S(2)}, u32[]{:S(2)}) collective-permute-start(f32[2,32,128]{2,1,0:T(8,128)S(1)} %get-tuple-element.781), channel_id=1, source_target_pairs={{4,0},{8,4},{12,8},{16,12},{20,16},{24,20},{28,24},{0,28},{5,1},{9... | collective-permute-start | bytes 98312 | tf_op jit(solution)/shard_map/while/body/eval_jaxpr/ppermute | solution.py:21
  102.4 8.8 %collective-permute-start = (f32[2,32,128]{2,1,0:T(8,128)S(1)}, f32[2,32,128]{2,1,0:T(8,128)S(1)}, u32[]{:S(2)}, u32[]{:S(2)}) collective-permute-start(f32[2,32,128]{2,1,0:T(8,128)S(1)} %get-tuple-element.780), channel_id=1, source_target_pairs={{0,4},{4,8},{8,12},{12,16},{16,20},{20,24},{24,28},{28,0},{1,5},{5... | collective-permute-start | bytes 98312 | tf_op jit(solution)/shard_map/while/body/eval_jaxpr/ppermute | solution.py:18
  102.4 8.7 %collective-permute-start.1 = (f32[2,32,128]{2,1,0:T(8,128)S(1)}, f32[2,32,128]{2,1,0:T(8,128)S(1)}, u32[]{:S(2)}, u32[]{:S(2)}) collective-permute-start(f32[2,32,128]{2,1,0:T(8,128)S(1)} %get-tuple-element.781), channel_id=1, source_target_pairs={{4,0},{8,4},{12,8},{16,12},{20,16},{24,20},{28,24},{0,28},{5,1},{9... | collective-permute-start | bytes 98312 | tf_op jit(solution)/shard_map/while/body/eval_jaxpr/ppermute | solution.py:21
  118.8 8.8 %collective-permute-start = (f32[2,32,128]{2,1,0:T(8,128)S(1)}, f32[2,32,128]{2,1,0:T(8,128)S(1)}, u32[]{:S(2)}, u32[]{:S(2)}) collective-permute-start(f32[2,32,128]{2,1,0:T(8,128)S(1)} %get-tuple-element.780), channel_id=1, source_target_pairs={{0,4},{4,8},{8,12},{12,16},{16,20},{20,24},{24,28},{28,0},{1,5},{5... | collective-permute-start | bytes 98312 | tf_op jit(solution)/shard_map/while/body/eval_jaxpr/ppermute | solution.py:18
  118.8 8.7 %collective-permute-start.1 = (f32[2,32,128]{2,1,0:T(8,128)S(1)}, f32[2,32,128]{2,1,0:T(8,128)S(1)}, u32[]{:S(2)}, u32[]{:S(2)}) collective-permute-start(f32[2,32,128]{2,1,0:T(8,128)S(1)} %get-tuple-element.781), channel_id=1, source_target_pairs={{4,0},{8,4},{12,8},{16,12},{20,16},{24,20},{28,24},{0,28},{5,1},{9... | collective-permute-start | bytes 98312 | tf_op jit(solution)/shard_map/while/body/eval_jaxpr/ppermute | solution.py:21
  135.2 8.8 %collective-permute-start = (f32[2,32,128]{2,1,0:T(8,128)S(1)}, f32[2,32,128]{2,1,0:T(8,128)S(1)}, u32[]{:S(2)}, u32[]{:S(2)}) collective-permute-start(f32[2,32,128]{2,1,0:T(8,128)S(1)} %get-tuple-element.780), channel_id=1, source_target_pairs={{0,4},{4,8},{8,12},{12,16},{16,20},{20,24},{24,28},{28,0},{1,5},{5... | collective-permute-start | bytes 98312 | tf_op jit(solution)/shard_map/while/body/eval_jaxpr/ppermute | solution.py:18
  135.2 8.7 %collective-permute-start.1 = (f32[2,32,128]{2,1,0:T(8,128)S(1)}, f32[2,32,128]{2,1,0:T(8,128)S(1)}, u32[]{:S(2)}, u32[]{:S(2)}) collective-permute-start(f32[2,32,128]{2,1,0:T(8,128)S(1)} %get-tuple-element.781), channel_id=1, source_target_pairs={{4,0},{8,4},{12,8},{16,12},{20,16},{24,20},{28,24},{0,28},{5,1},{9... | collective-permute-start | bytes 98312 | tf_op jit(solution)/shard_map/while/body/eval_jaxpr/ppermute | solution.py:21
  151.6 8.8 %collective-permute-start = (f32[2,32,128]{2,1,0:T(8,128)S(1)}, f32[2,32,128]{2,1,0:T(8,128)S(1)}, u32[]{:S(2)}, u32[]{:S(2)}) collective-permute-start(f32[2,32,128]{2,1,0:T(8,128)S(1)} %get-tuple-element.780), channel_id=1, source_target_pairs={{0,4},{4,8},{8,12},{12,16},{16,20},{20,24},{24,28},{28,0},{1,5},{5... | collective-permute-start | bytes 98312 | tf_op jit(solution)/shard_map/while/body/eval_jaxpr/ppermute | solution.py:18
  168.0 8.8 %collective-permute-start = (f32[2,32,128]{2,1,0:T(8,128)S(1)}, f32[2,32,128]{2,1,0:T(8,128)S(1)}, u32[]{:S(2)}, u32[]{:S(2)}) collective-permute-start(f32[2,32,128]{2,1,0:T(8,128)S(1)} %get-tuple-element.780), channel_id=1, source_target_pairs={{0,4},{4,8},{8,12},{12,16},{16,20},{20,24},{24,28},{28,0},{1,5},{5... | collective-permute-start | bytes 98312 | tf_op jit(solution)/shard_map/while/body/eval_jaxpr/ppermute | solution.py:18
  184.4 8.8 %collective-permute-start = (f32[2,32,128]{2,1,0:T(8,128)S(1)}, f32[2,32,128]{2,1,0:T(8,128)S(1)}, u32[]{:S(2)}, u32[]{:S(2)}) collective-permute-start(f32[2,32,128]{2,1,0:T(8,128)S(1)} %get-tuple-element.780), channel_id=1, source_target_pairs={{0,4},{4,8},{8,12},{12,16},{16,20},{20,24},{24,28},{28,0},{1,5},{5... | collective-permute-start | bytes 98312 | tf_op jit(solution)/shard_map/while/body/eval_jaxpr/ppermute | solution.py:18
  200.8 8.8 %collective-permute-start = (f32[2,32,128]{2,1,0:T(8,128)S(1)}, f32[2,32,128]{2,1,0:T(8,128)S(1)}, u32[]{:S(2)}, u32[]{:S(2)}) collective-permute-start(f32[2,32,128]{2,1,0:T(8,128)S(1)} %get-tuple-element.780), channel_id=1, source_target_pairs={{0,4},{4,8},{8,12},{12,16},{16,20},{20,24},{24,28},{28,0},{1,5},{5... | collective-permute-start | bytes 98312 | tf_op jit(solution)/shard_map/while/body/eval_jaxpr/ppermute | solution.py:18
  200.8 8.7 %collective-permute-start.1 = (f32[2,32,128]{2,1,0:T(8,128)S(1)}, f32[2,32,128]{2,1,0:T(8,128)S(1)}, u32[]{:S(2)}, u32[]{:S(2)}) collective-permute-start(f32[2,32,128]{2,1,0:T(8,128)S(1)} %get-tuple-element.781), channel_id=1, source_target_pairs={{4,0},{8,4},{12,8},{16,12},{20,16},{24,20},{28,24},{0,28},{5,1},{9... | collective-permute-start | bytes 98312 | tf_op jit(solution)/shard_map/while/body/eval_jaxpr/ppermute | solution.py:21
  217.2 8.8 %collective-permute-start = (f32[2,32,128]{2,1,0:T(8,128)S(1)}, f32[2,32,128]{2,1,0:T(8,128)S(1)}, u32[]{:S(2)}, u32[]{:S(2)}) collective-permute-start(f32[2,32,128]{2,1,0:T(8,128)S(1)} %get-tuple-element.780), channel_id=1, source_target_pairs={{0,4},{4,8},{8,12},{12,16},{16,20},{20,24},{24,28},{28,0},{1,5},{5... | collective-permute-start | bytes 98312 | tf_op jit(solution)/shard_map/while/body/eval_jaxpr/ppermute | solution.py:18
  217.2 8.7 %collective-permute-start.1 = (f32[2,32,128]{2,1,0:T(8,128)S(1)}, f32[2,32,128]{2,1,0:T(8,128)S(1)}, u32[]{:S(2)}, u32[]{:S(2)}) collective-permute-start(f32[2,32,128]{2,1,0:T(8,128)S(1)} %get-tuple-element.781), channel_id=1, source_target_pairs={{4,0},{8,4},{12,8},{16,12},{20,16},{24,20},{28,24},{0,28},{5,1},{9... | collective-permute-start | bytes 98312 | tf_op jit(solution)/shard_map/while/body/eval_jaxpr/ppermute | solution.py:21
  233.6 8.8 %collective-permute-start = (f32[2,32,128]{2,1,0:T(8,128)S(1)}, f32[2,32,128]{2,1,0:T(8,128)S(1)}, u32[]{:S(2)}, u32[]{:S(2)}) collective-permute-start(f32[2,32,128]{2,1,0:T(8,128)S(1)} %get-tuple-element.780), channel_id=1, source_target_pairs={{0,4},{4,8},{8,12},{12,16},{16,20},{20,24},{24,28},{28,0},{1,5},{5... | collective-permute-start | bytes 98312 | tf_op jit(solution)/shard_map/while/body/eval_jaxpr/ppermute | solution.py:18
  233.6 8.7 %collective-permute-start.1 = (f32[2,32,128]{2,1,0:T(8,128)S(1)}, f32[2,32,128]{2,1,0:T(8,128)S(1)}, u32[]{:S(2)}, u32[]{:S(2)}) collective-permute-start(f32[2,32,128]{2,1,0:T(8,128)S(1)} %get-tuple-element.781), channel_id=1, source_target_pairs={{4,0},{8,4},{12,8},{16,12},{20,16},{24,20},{28,24},{0,28},{5,1},{9... | collective-permute-start | bytes 98312 | tf_op jit(solution)/shard_map/while/body/eval_jaxpr/ppermute | solution.py:21
  250.0 8.8 %collective-permute-start = (f32[2,32,128]{2,1,0:T(8,128)S(1)}, f32[2,32,128]{2,1,0:T(8,128)S(1)}, u32[]{:S(2)}, u32[]{:S(2)}) collective-permute-start(f32[2,32,128]{2,1,0:T(8,128)S(1)} %get-tuple-element.780), channel_id=1, source_target_pairs={{0,4},{4,8},{8,12},{12,16},{16,20},{20,24},{24,28},{28,0},{1,5},{5... | collective-permute-start | bytes 98312 | tf_op jit(solution)/shard_map/while/body/eval_jaxpr/ppermute | solution.py:18
  250.0 8.7 %collective-permute-start.1 = (f32[2,32,128]{2,1,0:T(8,128)S(1)}, f32[2,32,128]{2,1,0:T(8,128)S(1)}, u32[]{:S(2)}, u32[]{:S(2)}) collective-permute-start(f32[2,32,128]{2,1,0:T(8,128)S(1)} %get-tuple-element.781), channel_id=1, source_target_pairs={{4,0},{8,4},{12,8},{16,12},{20,16},{24,20},{28,24},{0,28},{5,1},{9... | collective-permute-start | bytes 98312 | tf_op jit(solution)/shard_map/while/body/eval_jaxpr/ppermute | solution.py:21
  303.6 9.6 %collective-permute-start.6 = (f32[2,32,128]{2,1,0:T(8,128)S(1)}, f32[2,32,128]{2,1,0:T(8,128)S(1)}, u32[]{:S(2)}, u32[]{:S(2)}) collective-permute-start(f32[2,32,128]{2,1,0:T(8,128)S(1)} %get-tuple-element.798), channel_id=1, source_target_pairs={{0,4},{4,8},{8,12},{12,16},{16,20},{20,24},{24,28},{28,0},{1,5},{5... | collective-permute-start | bytes 98312 | tf_op jit(solution)/shard_map/while/body/eval_jaxpr/ppermute | solution.py:18
  307.9 10.0 %collective-permute-start.8 = (f32[4,32,2]{2,1,0:T(8,128)S(1)}, f32[4,32,2]{2,1,0:T(8,128)S(1)}, u32[]{:S(2)}, u32[]{:S(2)}) collective-permute-start(f32[4,32,2]{2,1,0:T(8,128)S(1)} %get-tuple-element.800), channel_id=1, source_target_pairs={{0,1},{2,3},{4,5},{6,7},{8,9},{10,11},{12,13},{14,15},{16,17},{18,... | collective-permute-start | bytes 3080 | tf_op jit(solution)/shard_map/while/body/eval_jaxpr/ppermute | solution.py:18
  309.2 8.7 %collective-permute-start.9 = (f32[4,32,2]{2,1,0:T(8,128)S(1)}, f32[4,32,2]{2,1,0:T(8,128)S(1)}, u32[]{:S(2)}, u32[]{:S(2)}) collective-permute-start(f32[4,32,2]{2,1,0:T(8,128)S(1)} %get-tuple-element.801), channel_id=1, source_target_pairs={{1,0},{3,2},{5,4},{7,6},{9,8},{11,10},{13,12},{15,14},{17,16},{19,... | collective-permute-start | bytes 3080 | tf_op jit(solution)/shard_map/while/body/eval_jaxpr/ppermute | solution.py:21
  334.4 8.7 %collective-permute-start.6 = (f32[2,32,128]{2,1,0:T(8,128)S(1)}, f32[2,32,128]{2,1,0:T(8,128)S(1)}, u32[]{:S(2)}, u32[]{:S(2)}) collective-permute-start(f32[2,32,128]{2,1,0:T(8,128)S(1)} %get-tuple-element.798), channel_id=1, source_target_pairs={{0,4},{4,8},{8,12},{12,16},{16,20},{20,24},{24,28},{28,0},{1,5},{5... | collective-permute-start | bytes 98312 | tf_op jit(solution)/shard_map/while/body/eval_jaxpr/ppermute | solution.py:18
  (181 other events, 1167.5 us)
where the time goes:
time: 782 us; the launch traced here: 776 us
  starting transfers between devices  327 us (42%)
  other arithmetic  280 us (36%)
  loops' own time  67.4 us (9%)
  local copies, waits for them, and re-layouts  61.1 us (8%)
  blocking collectives  39.7 us (5%)
    scatter-add x16, other arithmetic, adjoint_step(): adjoint = adjoint.at[clip_x, clip_y, clip_z].add(inject)  246 us
    ppermute x96, starting transfers between devices, with_halo(): lax.ppermute(lax.slice_in_dim(block, 0, width, axis=dim), axis, backward)  238 us
    ppermute x96, starting transfers between devices, with_halo(): lax.ppermute(lax.slice_in_dim(block, block.shape[dim] - width, None, axis...  89 us
    gather x16, local copies, waits for them, and re-layouts, sample_row(): values = field[clip_x, clip_y, clip_z] * inside  37.9 us
    psum x1, blocking collectives, on_device(): traces = lax.psum(record, ('gx', 'gy', 'gz'))  37.1 us
    another operation x1, loops' own time, on_device(): lax.fori_loop(0, steps, adjoint_step, (zeros, zeros, zeros))  33.8 us
    another operation x1, loops' own time, on_device(): lax.fori_loop(0, steps, forward, (zeros, zeros, record))  33.7 us
  transfers between devices with their start and end apart: 192, of which 0 were waited for; matrix products, arithmetic and copies ran while one was open for 3% of the time, Pallas kernels for 0%

commit v1 on v0

--- a/solution.py
+++ b/solution.py
@@ -1,6 +1,10 @@
+import functools
+
 import jax
 import jax.numpy as jnp
 from jax import lax
+from jax.experimental import pallas as pl
+from jax.experimental.pallas import tpu as pltpu
 from jax.sharding import PartitionSpec as P
 
 near_coef = 4.0 / 3.0
@@ -97,12 +101,505 @@
     return (image, traces, column_image, current)
 
 
+MESH = pl.DeviceIdType.MESH
+BLOCK = 4
+GROUP = 4
+
+
+def place_of(p, gxs, gys, gzs):
+    q, gz = p // gzs, p % gzs
+    per = 2 * gys
+    zz, w = q // per, q % per
+    w = w + (zz % 2) * (per - 1 - 2 * w)
+    xx, yy = w // gys, w % gys
+    return 2 * zz + xx, yy + xx * (gys - 1 - 2 * yy), gz
+
+
+def position_of(gx, gy, gz, gxs, gys, gzs):
+    per = 2 * gys
+    zz, xx = gx // 2, gx % 2
+    w = xx * gys + gy + xx * (gys - 1 - 2 * gy)
+    w = w + (zz % 2) * (per - 1 - 2 * w)
+    return (zz * per + w) * gzs + gz
+
+
+def lateral(f, sx, sy, gys):
+    rows, lanes = f.shape[1], f.shape[2]
+    lane = lax.broadcasted_iota(jnp.int32, f.shape, 2)
+    row = lax.broadcasted_iota(jnp.int32, f.shape, 1)
+    yl = lane % sy
+
+    def rr(a, k):
+        return pltpu.roll(a, k % rows, 1) if k % rows else a
+
+    def lr(a, k):
+        return pltpu.roll(a, k % lanes, 2) if k % lanes else a
+
+    gy = row % gys
+    up = jnp.where(gy == gys - 1, rr(f, gys - 1), rr(f, -1))
+    down = up if gys == 2 else jnp.where(gy == 0, rr(f, 1 - gys), rr(f, 1))
+    fu, fd = lr(up, sy), lr(down, -sy)
+    y1 = lr(jnp.where(yl >= 1, f, fu), -1) + lr(jnp.where(yl < sy - 1, f, fd), 1)
+    y2 = lr(jnp.where(yl >= 2, f, fu), -2) + lr(jnp.where(yl < sy - 2, f, fd), 2)
+    xu, xd = rr(f, -gys), rr(f, gys)
+    x1 = lr(jnp.where(lane >= sy, f, xu), -sy) + lr(jnp.where(lane < lanes - sy, f, xd), sy)
+    x2 = lr(jnp.where(lane >= 2 * sy, f, xu), -2 * sy) + lr(jnp.where(lane < lanes - 2 * sy, f, xd), 2 * sy)
+    return near_coef * (x1 + y1) + far_coef * (x2 + y2)
+
+
+def chain_kernel(
+    dims, v_ref, m_ref, bg_ref, rec_ref, ck_ref,
+    image_ref, traces_ref, column_ref, wave_ref,
+    stage, landed, coef, own_bg, hist, adj, wbuf, img, count, fr, part, tr1, tr2, back_w, back_i, in_w, in_i,
+    s_in, r_in, s_c, r_c, s_f, r_f, s_t, r_t, s_w, r_w, s_i, r_i,
+):
+    gxs, gys, gzs, sx, sy, sz, nck, steps = dims
+    n = gxs * gys * gzs
+    rows = gxs * gys
+    lanes = sx * sy
+    nz = sz * gzs // n
+    per = sz // nz
+    fields = 2 + nck
+    gx, gy, gz = lax.axis_index("gx"), lax.axis_index("gy"), lax.axis_index("gz")
+    pos = position_of(gx, gy, gz, gxs, gys, gzs)
+    my_row = gx * gys + gy
+    lo_id = place_of(jnp.maximum(pos - 1, 0), gxs, gys, gzs)
+    hi_id = place_of(jnp.minimum(pos + 1, n - 1), gxs, gys, gzs)
+    has_lo, has_hi = pos > 0, pos < n - 1
+    ext = 3 * nz
+    near_halo = 2 * (BLOCK - 1)
+
+    def remote(src, dst, ss, rs, where):
+        return pltpu.make_async_remote_copy(
+            src_ref=src, dst_ref=dst, send_sem=ss, recv_sem=rs, device_id=where, device_id_type=MESH
+        )
+
+    fr[...] = jnp.zeros_like(fr)
+    for f in range(1 + nck):
+        coef[f, 0:nz] = jnp.zeros((nz, rows, lanes), jnp.float32)
+        coef[f, 2 * nz :] = jnp.zeros((nz, rows, lanes), jnp.float32)
+
+    barrier = pltpu.get_barrier_semaphore()
+
+    def greet(p, carry):
+        @pl.when(p != pos)
+        def _():
+            pl.semaphore_signal(barrier, inc=1, device_id=place_of(p, gxs, gys, gzs), device_id_type=MESH)
+        return carry
+
+    lax.fori_loop(0, n, greet, 0)
+
+    for f in range(fields):
+        if f == 0:
+            block = v_ref[...]
+        elif f == 1:
+            block = m_ref[...]
+        else:
+            block = bg_ref[f - 2].astype(jnp.float32)
+        turned = block.reshape(lanes, sz).T
+        stage[:, f * nz : (f + 1) * nz, :] = turned.reshape(per, nz, lanes)
+    pl.semaphore_wait(barrier, n - 1)
+
+    slab = fields * nz
+
+    def arrival(row):
+        return landed.at[pl.ds(pl.multiple_of(row * slab, nz), slab)]
+
+    def scatter_in(c, carry):
+        p = gz * per + c
+
+        @pl.when(p != pos)
+        def _():
+            remote(stage.at[c], arrival(my_row), s_in.at[c], r_in.at[my_row], place_of(p, gxs, gys, gzs)).start()
+
+        @pl.when(p == pos)
+        def _():
+            landed[pl.ds(pl.multiple_of(my_row * slab, nz), slab), :] = stage[c]
+
+        return carry
+
+    lax.fori_loop(0, per, scatter_in, 0)
+
+    rec = rec_ref[...]
+    rx, ry, rz = rec[0:1], rec[1:2], rec[2:3]
+    nrec = rec.shape[1]
+    rrow = (rx // sx) * gys + ry // sy
+    rlane = (rx % sx) * sy + ry % sy
+    rlocal = rz - (pos - 1) * nz
+    zr = jnp.where((rlocal >= 0) & (rlocal < ext), rlocal * rows + rrow, -1)
+    one_zr = (lax.broadcasted_iota(jnp.int32, (ext * rows, nrec), 0) == zr).astype(jnp.float32)
+    one_lane = (lax.broadcasted_iota(jnp.int32, (lanes, nrec), 0) == rlane).astype(jnp.float32)
+    counted = lax.dot_general(
+        one_zr.astype(jnp.bfloat16), one_lane.astype(jnp.bfloat16), (((1,), (1,)), ((), ())),
+        preferred_element_type=jnp.float32,
+    )
+    count[...] = counted.reshape(ext, rows, lanes)
+    hist[0] = jnp.zeros((ext, rows, lanes), jnp.float32)
+    hist[1] = jnp.zeros((ext, rows, lanes), jnp.float32)
+    adj[steps] = jnp.zeros((ext, rows, lanes), jnp.float32)
+    adj[steps + 1] = jnp.zeros((ext, rows, lanes), jnp.float32)
+    img[...] = jnp.zeros_like(img)
+
+    owner = pos // per
+
+    def wait_in(row, carry):
+        sender = row // gys, row % gys, owner
+
+        @pl.when((row != my_row) | (owner != gz))
+        def _():
+            remote(stage.at[0], arrival(row), s_in.at[0], r_in.at[row], sender).wait_recv()
+
+        return carry
+
+    lax.fori_loop(0, rows, wait_in, 0)
+
+    def sent_in(c, carry):
+        @pl.when(gz * per + c != pos)
+        def _():
+            remote(stage.at[c], arrival(my_row), s_in.at[c], r_in.at[my_row], lo_id).wait_send()
+
+        return carry
+
+    lax.fori_loop(0, per, sent_in, 0)
+
+    for z in range(nz):
+        def plane(f):
+            return landed[pl.ds(f * nz + z, rows, stride=slab), :]
+
+        coef[0, nz + z] = plane(0)
+        model = plane(1)
+        for k in range(nck):
+            accel = plane(2 + k)
+            own_bg[k, z] = accel
+            coef[1 + k, nz + z] = model * accel
+
+    def coef_copies():
+        v_lo = remote(coef.at[0, pl.ds(nz, nz)], coef.at[0, pl.ds(2 * nz, nz)], s_c.at[0], r_c.at[0], lo_id)
+        m_lo = remote(
+            coef.at[pl.ds(1, nck), pl.ds(nz, near_halo)], coef.at[pl.ds(1, nck), pl.ds(2 * nz, near_halo)],
+            s_c.at[1], r_c.at[1], lo_id,
+        )
+        v_hi = remote(coef.at[0, pl.ds(nz, nz)], coef.at[0, pl.ds(0, nz)], s_c.at[2], r_c.at[2], hi_id)
+        m_hi = remote(
+            coef.at[pl.ds(1, nck), pl.ds(2 * nz - near_halo, near_halo)],
+            coef.at[pl.ds(1, nck), pl.ds(nz - near_halo, near_halo)],
+            s_c.at[3], r_c.at[3], hi_id,
+        )
+        return (m_lo, v_lo), (m_hi, v_hi)
+
+    def field_copies(e, newer, older):
+        to_lo = [
+            remote(a.at[pl.ds(nz, nz)], fr.at[e, 1, i], s_f.at[e, 0, i], r_f.at[e, 1, i], lo_id)
+            for i, a in enumerate((newer, older))
+        ]
+        to_hi = [
+            remote(a.at[pl.ds(nz, nz)], fr.at[e, 0, i], s_f.at[e, 1, i], r_f.at[e, 0, i], hi_id)
+            for i, a in enumerate((newer, older))
+        ]
+        return to_lo, to_hi
+
+    def launch(copies):
+        to_lo, to_hi = copies
+
+        @pl.when(has_hi)
+        def _():
+            for c in to_hi:
+                c.start()
+
+        @pl.when(has_lo)
+        def _():
+            for c in to_lo:
+                c.start()
+
+    def settle(copies):
+        to_lo, to_hi = copies
+
+        @pl.when(has_hi)
+        def _():
+            for c in to_lo:
+                c.wait_recv()
+            for c in to_hi:
+                c.wait_send()
+
+        @pl.when(has_lo)
+        def _():
+            for c in to_hi:
+                c.wait_recv()
+            for c in to_lo:
+                c.wait_send()
+
+    def fill(e, newer, older):
+        for i, a in enumerate((newer, older)):
+            a[0:nz] = fr[e, 0, i]
+            a[2 * nz :] = fr[e, 1, i]
+
+    def stencil(ref, at, size):
+        f = ref[pl.ds(at, size)]
+        first = ref[pl.ds(at + 1, size)] + ref[pl.ds(at - 1, size)]
+        second = ref[pl.ds(at + 2, size)] + ref[pl.ds(at - 2, size)]
+        return 3.0 * center_coef * f + lateral(f, sx, sy, gys) + near_coef * first + far_coef * second, f
+
+    copies = coef_copies()
+    launch(copies)
+    settle(copies)
+
+    def forward_block(b, carry):
+        for j in range(BLOCK):
+            step = b * BLOCK + j
+            ck = ck_ref[step]
+            lo = 2 * (j + 1)
+            for at in range(lo, ext - lo, GROUP):
+                size = min(GROUP, ext - lo - at)
+                lap, f = stencil(hist.at[step + 1], at, size)
+                src = coef[1 + ck, at : at + size]
+                hist[step + 2, at : at + size] = (
+                    2.0 * f - hist[step, at : at + size] + coef[0, at : at + size] * lap + src
+                )
+        newer, older = hist.at[(b + 1) * BLOCK + 1], hist.at[(b + 1) * BLOCK]
+        moves = field_copies(b, newer, older)
+        launch(moves)
+        settle(moves)
+        fill(b, newer, older)
+        return carry
+
+    blocks = steps // BLOCK
+    lax.fori_loop(0, blocks, forward_block, 0)
+
+    def send_back(src, dst, ss, rs, slot, g):
+        def one(row, carry):
+            other = (row != my_row) | (g != gz)
+
+            @pl.when(other)
+            def _():
+                remote(src.at[row], dst.at[slot], ss.at[row], rs.at[slot], (row // gys, row % gys, g)).start()
+
+            @pl.when(jnp.logical_not(other))
+            def _():
+                dst[slot] = src[row]
+
+            return carry
+
+        lax.fori_loop(0, rows, one, 0)
+
+    def sent_back(src, dst, ss, rs, g):
+        def one(row, carry):
+            @pl.when((row != my_row) | (g != gz))
+            def _():
+                remote(src.at[row], dst.at[0], ss.at[row], rs.at[0], lo_id).wait_send()
+
+            return carry
+
+        lax.fori_loop(0, rows, one, 0)
+
+    def got_back(src, dst, ss, rs, first, number):
+        def one(c, carry):
+            @pl.when(c + first != pos)
+            def _():
+                remote(src.at[0], dst.at[c], ss.at[0], rs.at[c], lo_id).wait_recv()
+
+            return carry
+
+        lax.fori_loop(0, number, one, 0)
+
+    near = 4
+    far = n // near
+    team, seat = pos // near, pos % near
+
+    def trace_sends(src, dst, kind):
+        number = near if kind == 0 else far
+        mine = seat if kind == 0 else team
+
+        def one(i, carry):
+            @pl.when(i != mine)
+            def _():
+                p = team * near + i if kind == 0 else i * near + seat
+                remote(src, dst.at[mine], s_t.at[kind, i], r_t.at[kind, mine], place_of(p, gxs, gys, gzs)).start()
+
+            return carry
+
+        lax.fori_loop(0, number, one, 0)
+
+    def trace_waits(src, dst, kind):
+        number = near if kind == 0 else far
+        mine = seat if kind == 0 else team
+
+        def one(i, carry):
+            @pl.when(i != mine)
+            def _():
+                remote(src, dst.at[i], s_t.at[kind, i], r_t.at[kind, i], lo_id).wait()
+
+            return carry
+
+        lax.fori_loop(0, number, one, 0)
+
+    def gather_traces():
+        picked = one_zr[nz * rows : 2 * nz * rows]
+        lines = []
+        for t in range(steps):
+            table = hist[t + 2, nz : 2 * nz].reshape(nz * rows, lanes)
+            at_lane = lax.dot_general(
+                table, picked, (((0,), (0,)), ((), ())),
+                preferred_element_type=jnp.float32, precision=lax.Precision.HIGHEST,
+            )
+            lines.append(jnp.sum(at_lane * one_lane, axis=0, keepdims=True))
+        return jnp.concatenate(lines, axis=0)
+
+    def adjoint_block(b, carry):
+        for j in range(BLOCK):
+            step = steps - 1 - b * BLOCK - j
+            ck = ck_ref[step]
+            lo = 2 * (j + 1)
+            wbuf[lo - 2 : ext - lo + 2] = coef[0, lo - 2 : ext - lo + 2] * adj[step + 1, lo - 2 : ext - lo + 2]
+            for at in range(lo, ext - lo, GROUP):
+                size = min(GROUP, ext - lo - at)
+                lap, f = stencil(wbuf, at, size)
+                adj[step, at : at + size] = (
+                    2.0 * adj[step + 1, at : at + size] - adj[step + 2, at : at + size] + lap
+                    + count[at : at + size] * hist[step + 2, at : at + size]
+                )
+            img[...] += adj[step, nz : 2 * nz] * own_bg[ck]
+
+        @pl.when(b < blocks - 1)
+        def _():
+            newer, older = adj.at[steps - (b + 1) * BLOCK], adj.at[steps - (b + 1) * BLOCK + 1]
+            moves = field_copies(blocks + b, newer, older)
+            launch(moves)
+
+            @pl.when(b == 0)
+            def _():
+                part[0] = gather_traces()
+                tr1[seat] = part[0]
+                trace_sends(part.at[0], tr1, 0)
+                for row in range(rows):
+                    for z in range(nz):
+                        back_w[row, z : z + 1] = hist[steps + 1, nz + z, row : row + 1]
+                send_back(back_w, in_w, s_w, r_w, lax.rem(pos, per), owner)
+
+            @pl.when(b == 1)
+            def _():
+                trace_waits(part.at[0], tr1, 0)
+                total = tr1[0]
+                for i in range(1, near):
+                    total = total + tr1[i]
+                part[1] = total
+                tr2[team] = total
+                trace_sends(part.at[1], tr2, 1)
+
+            settle(moves)
+            fill(blocks + b, newer, older)
+
+        return carry
+
+    lax.fori_loop(0, blocks, adjoint_block, 0)
+
+    for row in range(rows):
+        for z in range(nz):
+            back_i[row, z : z + 1] = img[z, row : row + 1]
+    for g in range(gzs):
+        send_back(back_i, in_i, s_i.at[g], r_i, pos, g)
+
+    trace_waits(part.at[1], tr2, 1)
+    total = tr2[0]
+    for i in range(1, far):
+        total = total + tr2[i]
+    traces_ref[...] = total
+    got_back(back_w, in_w, s_w, r_w, gz * per, per)
+    wave_ref[...] = in_w[...].reshape(sz, lanes).T.reshape(sx, sy, sz)
+    sent_back(back_w, in_w, s_w, r_w, owner)
+
+    got_back(back_i, in_i, s_i.at[0], r_i, 0, n)
+    mine = in_i[pl.ds(gz * per, per)]
+    image_ref[...] = mine.reshape(sz, lanes).T.reshape(sx, sy, sz)
+    column_ref[...] = jnp.sum(in_i[...].reshape(n * nz, lanes), axis=0, keepdims=True) / (sz * gzs)
+    for g in range(gzs):
+        sent_back(back_i, in_i, s_i.at[g], r_i, g)
+
+
+def chain_on_device(sizes, velocity_term, model_step, background, receivers, checkpoints):
+    gxs, gys, gzs = sizes
+    sx, sy, sz = model_step.shape
+    nck, steps, nrec = background.shape[0], checkpoints.shape[0], receivers.shape[1]
+    n, rows, lanes = gxs * gys * gzs, gxs * gys, sx * sy
+    nz = sz * gzs // n
+    per = sz // nz
+    ext = 3 * nz
+    blocks = steps // BLOCK
+    dims = (gxs, gys, gzs, sx, sy, sz, nck, steps)
+    f32 = jnp.float32
+    dma = pltpu.SemaphoreType.DMA
+    vmem = pl.BlockSpec(memory_space=pltpu.VMEM)
+    image, traces, column, wave = pl.pallas_call(
+        functools.partial(chain_kernel, dims),
+        out_shape=(
+            jax.ShapeDtypeStruct((sx, sy, sz), f32),
+            jax.ShapeDtypeStruct((steps, nrec), f32),
+            jax.ShapeDtypeStruct((1, lanes), f32),
+            jax.ShapeDtypeStruct((sx, sy, sz), f32),
+        ),
+        in_specs=[vmem] * 4 + [pl.BlockSpec(memory_space=pltpu.SMEM)],
+        out_specs=(vmem,) * 4,
+        scratch_shapes=[
+            pltpu.VMEM((per, (2 + nck) * nz, lanes), f32),
+            pltpu.VMEM((rows * (2 + nck) * nz, lanes), f32),
+            pltpu.VMEM((1 + nck, ext, rows, lanes), f32),
+            pltpu.VMEM((nck, nz, rows, lanes), f32),
+            pltpu.VMEM((steps + 2, ext, rows, lanes), f32),
+            pltpu.VMEM((steps + 2, ext, rows, lanes), f32),
+            pltpu.VMEM((ext, rows, lanes), f32),
+            pltpu.VMEM((nz, rows, lanes), f32),
+            pltpu.VMEM((ext, rows, lanes), f32),
+            pltpu.VMEM((2 * blocks - 1, 2, 2, nz, rows, lanes), f32),
+            pltpu.VMEM((2, steps, nrec), f32),
+            pltpu.VMEM((4, steps, nrec), f32),
+            pltpu.VMEM((n // 4, steps, nrec), f32),
+            pltpu.VMEM((rows, nz, lanes), f32),
+            pltpu.VMEM((rows, nz, lanes), f32),
+            pltpu.VMEM((per, nz, lanes), f32),
+            pltpu.VMEM((n, nz, lanes), f32),
+            dma((per,)),
+            dma((rows,)),
+            dma((4,)),
+            dma((4,)),
+            dma((2 * blocks - 1, 2, 2)),
+            dma((2 * blocks - 1, 2, 2)),
+            dma((2, max(4, n // 4))),
+            dma((2, max(4, n // 4))),
+            dma((rows,)),
+            dma((per,)),
+            dma((gzs, rows)),
+            dma((n,)),
+        ],
+        compiler_params=pltpu.CompilerParams(
+            collective_id=0, has_side_effects=True, vmem_limit_bytes=48 * 1024 * 1024
+        ),
+    )(velocity_term, model_step, background, receivers, checkpoints)
+    return image, traces, column.reshape(sx, sy), wave
+
+
 def solution(mesh):
-    placed = (P("gx", "gy", "gz"), P("gx", "gy", "gz"), P(None, "gx", "gy", "gz"), P(), P())
-    return jax.shard_map(
-        on_device,
-        mesh=mesh,
-        in_specs=placed,
-        out_specs=(P("gx", "gy", "gz"), P(), P("gx", "gy"), P("gx", "gy", "gz")),
-        check_vma=False,
-    )
+    gxs, gys, gzs = mesh.shape["gx"], mesh.shape["gy"], mesh.shape["gz"]
+    n = gxs * gys * gzs
+
+    def whole(velocity_term, model_step, background, receivers, checkpoints):
+        nx, ny, depth = model_step.shape
+        fits = (
+            depth % (8 * n) == 0
+            and depth // n == 2 * BLOCK
+            and gxs % 2 == 0
+            and (gxs * gys) % 8 == 0
+            and n % 4 == 0
+            and (nx // gxs) * (ny // gys) % 128 == 0
+            and (ny // gys) % 8 == 0
+            and nx // gxs >= 4
+            and checkpoints.shape[0] % BLOCK == 0
+        )
+        body = functools.partial(chain_on_device, (gxs, gys, gzs)) if fits else on_device
+        return jax.shard_map(
+            body,
+            mesh=mesh,
+            in_specs=(P("gx", "gy", "gz"), P("gx", "gy", "gz"), P(None, "gx", "gy", "gz"), P(), P()),
+            out_specs=(P("gx", "gy", "gz"), P(), P("gx", "gy"), P("gx", "gy", "gz")),
+            check_vma=False,
+        )(velocity_term, model_step, background, receivers, checkpoints)
+
+    return whole

time: 782 us -> 82 us (0.10)
  starting transfers between devices: 327 us -> 0 us
  other arithmetic: 280 us -> 0.66 us
  Pallas kernels: 0 us -> 73.4 us
  loops' own time: 67.4 us -> 0 us
  local copies, waits for them, and re-layouts: 61.1 us -> 6.96 us
  blocking collectives: 39.7 us -> 0 us
    ppermute x192 -> x0, starting transfers between devices: 327 us -> none  [the longest x96 238 us: with_halo(): lax.ppermute(lax.slice_in_dim(block, 0, width, axis=dim), axis, backward)]
    scatter-add x16 -> x0, other arithmetic: 246 us -> none  [adjoint_step(): adjoint = adjoint.at[clip_x, clip_y, clip_z].add(inject)]
    pallas_call x0 -> x1, Pallas kernels: none -> 73.4 us  [chain_on_device(): pl.pallas_call(functools.partial(chain_kernel, dims), out_shape=(jax.Shap...]
    another operation x2 -> x0, loops' own time: 67.4 us -> none  [the longest x1 33.8 us: on_device(): lax.fori_loop(0, steps, adjoint_step, (zeros, zeros, zeros))]
    psum x2 -> x0, blocking collectives: 39.7 us -> none  [the longest x1 37.1 us: on_device(): traces = lax.psum(record, ('gx', 'gy', 'gz'))]
    gather x16 -> x0, local copies, waits for them, and re-layouts: 37.9 us -> none  [sample_row(): values = field[clip_x, clip_y, clip_z] * inside]
    add x48 -> x0, other arithmetic: 31 us -> none  [the longest x16 15.4 us: forward(): 2.0 * current - previous + velocity_term * laplace(current)]
    dynamic_slice x48 -> x0, local copies, waits for them, and re-layouts: 18.8 us -> none  [the longest x16 9.38 us: forward(): checkpoints[step]]
  transfers between devices with their start and end apart: 192 -> 0, of which waited for: 0 -> 0; matrix products, arithmetic and copies ran while one was open for 3% -> 0% of each run, Pallas kernels for 0% -> 0%
where the time goes in v1:
time: 82 us; the launch traced here: 81.7 us
  Pallas kernels  73.4 us (90%)
  local copies, waits for them, and re-layouts  6.96 us (8%)
    pallas_call x1, Pallas kernels, chain_on_device(): pl.pallas_call(functools.partial(chain_kernel, dims), out_shape=(jax.Shap...  73.4 us
    unnamed x13, local copies, waits for them, and re-layouts  5.78 us

profile of v1, /device:TPU:1, one launch (start us, length us, event | category | flops | bytes accessed | tf_op | source)
XLA Modules:
  0.0 81.7 jit_solution(16536089498099412087)
XLA Ops:
  0.6 0.0 copy-start
  0.6 0.9 %copy-done = bf16[4,4,32,128]{3,2,1,0:T(8,128)(2,1)S(1)} copy-done((bf16[4,4,32,128]{3,2,1,0:T(8,128)(2,1)S(1)}, bf16[4,4,32,128]{3,2,1,0:T(8,128)(2,1)}, u32[]{:S(2)}) %copy-start) | copy-done | bytes 131096
  1.5 0.0 copy-start.1
  1.5 0.8 %copy-done.1 = f32[4,32,128]{2,1,0:T(8,128)S(1)} copy-done((f32[4,32,128]{2,1,0:T(8,128)S(1)}, f32[4,32,128]{2,1,0:T(8,128)}, u32[]{:S(2)}) %copy-start.1) | copy-done | bytes 65560
  2.4 0.0 copy-start.2
  2.4 0.8 %copy-done.2 = f32[4,32,128]{2,1,0:T(8,128)S(1)} copy-done((f32[4,32,128]{2,1,0:T(8,128)S(1)}, f32[4,32,128]{2,1,0:T(8,128)}, u32[]{:S(2)}) %copy-start.2) | copy-done | bytes 65560
  3.2 0.0 copy-start.3
  3.2 0.7 copy-done.3
  3.9 0.0 copy-start.4
  3.9 0.7 copy-done.4
  4.6 73.4 %shard_map.84 = (f32[4,32,128]{2,1,0:T(8,128)S(1)}, f32[16,256]{1,0:T(8,128)S(1)}, f32[1,128]{1,0:T(1,128)S(1)}, f32[4,32,128]{2,1,0:T(8,128)S(1)}) custom-call(f32[4,32,128]{2,1,0:T(8,128)S(1)} %copy-done.1, f32[4,32,128]{2,1,0:T(8,128)S(1)} %copy-done.2, bf16[4,4,32,128]{3,2,1,0:T(8,128)(2,1)S(1)} %copy-done, s32[3,256]{1,0:T(4,128)S(1)} %copy-done.3, ...), custom_call_target="tpu_custom_call" | custom-call | tf_op jit(solution)/shard_map/pallas_call | solution.py:531
  78.0 0.5 broadcast.3
  78.5 0.7 reduce.3
  79.2 0.7 reshape.11
  79.8 0.6 copy.12
  80.5 0.6 copy.13
  81.1 0.6 copy.14
Async XLA Ops:
  0.6 0.9 %copy-start = (bf16[4,4,32,128]{3,2,1,0:T(8,128)(2,1)S(1)}, bf16[4,4,32,128]{3,2,1,0:T(8,128)(2,1)}, u32[]{:S(2)}) copy-start(bf16[4,4,32,128]{3,2,1,0:T(8,128)(2,1)} %bg_ref.1) | copy-start | bytes 393220
  1.5 0.8 %copy-start.1 = (f32[4,32,128]{2,1,0:T(8,128)S(1)}, f32[4,32,128]{2,1,0:T(8,128)}, u32[]{:S(2)}) copy-start(f32[4,32,128]{2,1,0:T(8,128)} %v_ref.1) | copy-start | bytes 196612
  2.4 0.8 %copy-start.2 = (f32[4,32,128]{2,1,0:T(8,128)S(1)}, f32[4,32,128]{2,1,0:T(8,128)}, u32[]{:S(2)}) copy-start(f32[4,32,128]{2,1,0:T(8,128)} %m_ref.1) | copy-start | bytes 196612
  3.2 0.7 copy-start.3
  3.9 0.7 copy-start.4

commit v2 on v1

--- a/solution.py
+++ b/solution.py
@@ -103,7 +103,7 @@
 
 MESH = pl.DeviceIdType.MESH
 BLOCK = 4
-GROUP = 4
+GROUP = 1
 
 
 def place_of(p, gxs, gys, gzs):
@@ -148,10 +148,10 @@
 
 
 def chain_kernel(
-    dims, v_ref, m_ref, bg_ref, rec_ref, ck_ref,
+    dims, v_hbm, m_hbm, bg_hbm, rec_hbm, ck_hbm,
     image_ref, traces_ref, column_ref, wave_ref,
     stage, landed, coef, own_bg, hist, adj, wbuf, img, count, fr, part, tr1, tr2, back_w, back_i, in_w, in_i,
-    s_in, r_in, s_c, r_c, s_f, r_f, s_t, r_t, s_w, r_w, s_i, r_i,
+    v_ref, m_ref, bg_ref, rec_ref, ck_ref, s_a, s_in, r_in, s_c, r_c, s_f, r_f, s_t, r_t, s_w, r_w, s_i, r_i,
 ):
     gxs, gys, gzs, sx, sy, sz, nck, steps = dims
     n = gxs * gys * gzs
@@ -174,6 +174,15 @@
             src_ref=src, dst_ref=dst, send_sem=ss, recv_sem=rs, device_id=where, device_id_type=MESH
         )
 
+    fetches = [
+        pltpu.make_async_copy(src, dst, s_a.at[i])
+        for i, (src, dst) in enumerate(
+            ((v_hbm, v_ref), (m_hbm, m_ref), (bg_hbm, bg_ref), (rec_hbm, rec_ref), (ck_hbm, ck_ref))
+        )
+    ]
+    for fetch in fetches:
+        fetch.start()
+
     fr[...] = jnp.zeros_like(fr)
     for f in range(1 + nck):
         coef[f, 0:nz] = jnp.zeros((nz, rows, lanes), jnp.float32)
@@ -189,6 +198,8 @@
 
     lax.fori_loop(0, n, greet, 0)
 
+    for fetch in fetches:
+        fetch.wait()
     for f in range(fields):
         if f == 0:
             block = v_ref[...]
@@ -287,16 +298,17 @@
         )
         return (m_lo, v_lo), (m_hi, v_hi)
 
-    def field_copies(e, newer, older):
-        to_lo = [
-            remote(a.at[pl.ds(nz, nz)], fr.at[e, 1, i], s_f.at[e, 0, i], r_f.at[e, 1, i], lo_id)
-            for i, a in enumerate((newer, older))
-        ]
-        to_hi = [
-            remote(a.at[pl.ds(nz, nz)], fr.at[e, 0, i], s_f.at[e, 1, i], r_f.at[e, 0, i], hi_id)
-            for i, a in enumerate((newer, older))
-        ]
-        return to_lo, to_hi
+    def field_copies(e, field, older):
+        i = 1 if older else 0
+        near = near_halo if older else nz
+        to_lo = remote(
+            field.at[pl.ds(nz, near)], fr.at[e, 1, i, pl.ds(0, near)], s_f.at[e, 0, i], r_f.at[e, 1, i], lo_id
+        )
+        to_hi = remote(
+            field.at[pl.ds(2 * nz - near, near)], fr.at[e, 0, i, pl.ds(nz - near, near)],
+            s_f.at[e, 1, i], r_f.at[e, 0, i], hi_id,
+        )
+        return (to_lo,), (to_hi,)
 
     def launch(copies):
         to_lo, to_hi = copies
@@ -330,8 +342,9 @@
 
     def fill(e, newer, older):
         for i, a in enumerate((newer, older)):
-            a[0:nz] = fr[e, 0, i]
-            a[2 * nz :] = fr[e, 1, i]
+            near = near_halo if i else nz
+            a[nz - near : nz] = fr[e, 0, i, nz - near :]
+            a[2 * nz : 2 * nz + near] = fr[e, 1, i, :near]
 
     def stencil(ref, at, size):
         f = ref[pl.ds(at, size)]
@@ -344,6 +357,7 @@
     settle(copies)
 
     def forward_block(b, carry):
+        newer, older = hist.at[(b + 1) * BLOCK + 1], hist.at[(b + 1) * BLOCK]
         for j in range(BLOCK):
             step = b * BLOCK + j
             ck = ck_ref[step]
@@ -355,10 +369,11 @@
                 hist[step + 2, at : at + size] = (
                     2.0 * f - hist[step, at : at + size] + coef[0, at : at + size] * lap + src
                 )
-        newer, older = hist.at[(b + 1) * BLOCK + 1], hist.at[(b + 1) * BLOCK]
-        moves = field_copies(b, newer, older)
-        launch(moves)
-        settle(moves)
+            if j == BLOCK - 2:
+                launch(field_copies(b, older, True))
+        launch(field_copies(b, newer, False))
+        settle(field_copies(b, older, True))
+        settle(field_copies(b, newer, False))
         fill(b, newer, older)
         return carry
 
@@ -445,6 +460,7 @@
         return jnp.concatenate(lines, axis=0)
 
     def adjoint_block(b, carry):
+        newer, older = adj.at[steps - (b + 1) * BLOCK], adj.at[steps - (b + 1) * BLOCK + 1]
         for j in range(BLOCK):
             step = steps - 1 - b * BLOCK - j
             ck = ck_ref[step]
@@ -457,13 +473,23 @@
                     2.0 * adj[step + 1, at : at + size] - adj[step + 2, at : at + size] + lap
                     + count[at : at + size] * hist[step + 2, at : at + size]
                 )
-            img[...] += adj[step, nz : 2 * nz] * own_bg[ck]
+            if j == BLOCK - 2:
+
+                @pl.when(b < blocks - 1)
+                def _():
+                    launch(field_copies(blocks + b, older, True))
+
+            if j < BLOCK - 1:
+                img[...] += adj[step, nz : 2 * nz] * own_bg[ck]
 
         @pl.when(b < blocks - 1)
         def _():
-            newer, older = adj.at[steps - (b + 1) * BLOCK], adj.at[steps - (b + 1) * BLOCK + 1]
-            moves = field_copies(blocks + b, newer, older)
-            launch(moves)
+            launch(field_copies(blocks + b, newer, False))
+
+        img[...] += adj[step, nz : 2 * nz] * own_bg[ck]
+
+        @pl.when(b < blocks - 1)
+        def _():
 
             @pl.when(b == 0)
             def _():
@@ -485,7 +511,8 @@
                 tr2[team] = total
                 trace_sends(part.at[1], tr2, 1)
 
-            settle(moves)
+            settle(field_copies(blocks + b, older, True))
+            settle(field_copies(blocks + b, newer, False))
             fill(blocks + b, newer, older)
 
         return carry
@@ -510,9 +537,19 @@
     got_back(back_i, in_i, s_i.at[0], r_i, 0, n)
     mine = in_i[pl.ds(gz * per, per)]
     image_ref[...] = mine.reshape(sz, lanes).T.reshape(sx, sy, sz)
-    column_ref[...] = jnp.sum(in_i[...].reshape(n * nz, lanes), axis=0, keepdims=True) / (sz * gzs)
+    column = jnp.sum(in_i[...].reshape(n * nz, lanes), axis=0, keepdims=True) / (sz * gzs)
+    for x in range(sx):
+        column_ref[x : x + 1, :] = column[:, x * sy : (x + 1) * sy]
     for g in range(gzs):
         sent_back(back_i, in_i, s_i.at[g], r_i, g)
+
+
+def write_out(*refs):
+    copies = [pltpu.make_async_copy(refs[i], refs[4 + i], refs[8].at[i]) for i in range(4)]
+    for copy in copies:
+        copy.start()
+    for copy in copies:
+        copy.wait()
 
 
 def chain_on_device(sizes, velocity_term, model_step, background, receivers, checkpoints):
@@ -528,15 +565,16 @@
     f32 = jnp.float32
     dma = pltpu.SemaphoreType.DMA
     vmem = pl.BlockSpec(memory_space=pltpu.VMEM)
-    image, traces, column, wave = pl.pallas_call(
+    hbm = pl.BlockSpec(memory_space=pltpu.HBM)
+    results = pl.pallas_call(
         functools.partial(chain_kernel, dims),
         out_shape=(
             jax.ShapeDtypeStruct((sx, sy, sz), f32),
             jax.ShapeDtypeStruct((steps, nrec), f32),
-            jax.ShapeDtypeStruct((1, lanes), f32),
+            jax.ShapeDtypeStruct((sx, sy), f32),
             jax.ShapeDtypeStruct((sx, sy, sz), f32),
         ),
-        in_specs=[vmem] * 4 + [pl.BlockSpec(memory_space=pltpu.SMEM)],
+        in_specs=[hbm] * 5,
         out_specs=(vmem,) * 4,
         scratch_shapes=[
             pltpu.VMEM((per, (2 + nck) * nz, lanes), f32),
@@ -556,6 +594,12 @@
             pltpu.VMEM((rows, nz, lanes), f32),
             pltpu.VMEM((per, nz, lanes), f32),
             pltpu.VMEM((n, nz, lanes), f32),
+            pltpu.VMEM(velocity_term.shape, f32),
+            pltpu.VMEM(model_step.shape, f32),
+            pltpu.VMEM(background.shape, background.dtype),
+            pltpu.VMEM(receivers.shape, receivers.dtype),
+            pltpu.SMEM(checkpoints.shape, checkpoints.dtype),
+            dma((5,)),
             dma((per,)),
             dma((rows,)),
             dma((4,)),
@@ -570,10 +614,19 @@
             dma((n,)),
         ],
         compiler_params=pltpu.CompilerParams(
-            collective_id=0, has_side_effects=True, vmem_limit_bytes=48 * 1024 * 1024
+            collective_id=0, has_side_effects=True, vmem_limit_bytes=67043328
         ),
     )(velocity_term, model_step, background, receivers, checkpoints)
-    return image, traces, column.reshape(sx, sy), wave
+    return tuple(
+        pl.pallas_call(
+            write_out,
+            out_shape=tuple(jax.ShapeDtypeStruct(a.shape, a.dtype) for a in results),
+            in_specs=[vmem] * 4,
+            out_specs=(hbm,) * 4,
+            scratch_shapes=[dma((4,))],
+            compiler_params=pltpu.CompilerParams(vmem_limit_bytes=1024 * 1024),
+        )(*results)
+    )
 
 
 def solution(mesh):

time: 82 us -> 91.9 us (1.12)
  Pallas kernels: 73.4 us -> 87.9 us
  local copies, waits for them, and re-layouts: 6.96 us -> 3.04 us
    pallas_call x1, Pallas kernels: 73.4 us -> 87.2 us  [chain_on_device(): pl.pallas_call(functools.partial(chain_kernel, dims), out_shape=(jax.Shap...]
    unnamed x13 -> x8, local copies, waits for them, and re-layouts: 5.78 us -> 3.04 us
where the time goes in v2:
time: 91.9 us; the launch traced here: 91.6 us
  Pallas kernels  87.9 us (96%)
  local copies, waits for them, and re-layouts  3.04 us (3%)
    pallas_call x1, Pallas kernels, chain_on_device(): pl.pallas_call(functools.partial(chain_kernel, dims), out_shape=(jax.Shap...  87.2 us
    unnamed x8, local copies, waits for them, and re-layouts  3.04 us

profile of v2, /device:TPU:1, one launch (start us, length us, event | category | flops | bytes accessed | tf_op | source)
XLA Modules:
  0.0 91.6 jit_solution(1100659690478606770)
XLA Ops:
  0.6 87.2 %shard_map.84 = (f32[4,32,128]{2,1,0:T(8,128)}, f32[16,256]{1,0:T(8,128)}, f32[4,32]{1,0:T(4,128)}, f32[4,32,128]{2,1,0:T(8,128)}) custom-call(f32[4,32,128]{2,1,0:T(8,128)} %v_hbm.1, f32[4,32,128]{2,1,0:T(8,128)} %m_hbm.1, bf16[4,4,32,128]{3,2,1,0:T(8,128)(2,1)} %bg_hbm.1, s32[3,256]{1,0:T(4,128)} %rec_hbm.1, s32[16]{0:T(128)} %ck_hbm.1), custom_call_target="tpu_custom_call" | custom-call | tf_op jit(solution)/shard_map/pallas_call | solution.py:569
  87.8 0.0 copy-start.3
  87.8 0.6 copy-done.3
  88.5 0.0 copy-start
  88.5 0.8 copy-done
  89.3 0.0 copy-start.1
  89.3 0.8 copy-done.1
  90.2 0.0 copy-start.2
  90.2 0.7 copy-done.2
  90.9 0.7 shard_map.85
Async XLA Ops:
  87.8 0.7 copy-start.3
  88.5 0.8 copy-start
  89.3 0.8 copy-start.1
  90.2 0.7 copy-start.2
